TPU v7x, 32 devices: a whole 2x2x4 slice. The times are simulated.
32 devices in a mesh: seq: 8 (over y, x, core), mp: 4 (over z).
Axes of the slice: x: 2, y: 2, z: 4, core: 2. Of those that a mesh axis runs over, the one named last changes fastest.
Arguments:
- inputs: bfloat16 [8192, 4096], P('seq', 'mp'), may hold values from -6 to 6
- conv_weight: bfloat16 [4, 4096], P(None, 'mp'), may hold values from -3 to 3
- conv_bias: bfloat16 [4096], P('mp'), may hold values from -3 to 3
- doc_start: int32 [8192], P('seq'), may hold values from 0 to 8191, as said below
- counts: int32 [8], P('seq'), may hold values from 341 to 1024
Outputs:
- gram: float32 [4096, 4096], P('seq', 'mp')
Inputs may be any that keep to these rules, and one draw needn't show every extreme that they name: doc_start is never above the token's own position, and for t > 0 either doc_start[t] == t or doc_start[t] == doc_start[t - 1]; doc_start[0] is 0.
All inputs are finite; a program needn't handle non-finite values.
Results may differ from a plain program's by a relative error of at most 0.0003.
Values may be sent and summed in bfloat16 or wider, within the bound.
A program may use at most 64 MiB of HBM per device.

v0:
```python
import functools

import jax
import jax.numpy as jnp
from jax import lax
from jax.experimental import pallas as pl
from jax.experimental.pallas import tpu as pltpu
from jax.sharding import PartitionSpec as P

MESH = pl.DeviceIdType.MESH
LANES = 128
HALO = 16


def when(cond):
    return pl.when(cond)


def gram_kernel(peers, depth, taps, x_hbm, taps_ref, code_ref, cnt_ref, o_ref, ext, feats, got, part,
                from_x, from_y, sum_y, sum_x, totals,
                load_sem, halo_sem, cnt_send, cnt_recv, pair_send, pair_recv,
                up_send, down_send, fwd_send, got_recv,
                a1_send, a1_recv, b1_send, b1_recv, a2_send, a2_recv, b2_send, b2_recv):
    s, z = lax.axis_index("seq"), lax.axis_index("mp")
    core, x, y = lax.rem(s, 2), lax.rem(s // 2, 2), s // 4
    sib, over_x, over_y = s + 1 - 2 * core, s + 2 - 4 * x, s + 4 - 8 * y
    quad = s // 2
    rows, width = x_hbm.shape
    half = width // 2
    pieces = half // LANES

    def remote(src, dst, send, recv, to):
        return pltpu.make_async_remote_copy(src_ref=src, dst_ref=dst, send_sem=send, recv_sem=recv,
                                            device_id=to, device_id_type=MESH)

    load = pltpu.make_async_copy(x_hbm, ext.at[pl.ds(HALO, rows)], load_sem)
    load.start()

    barrier = pltpu.get_barrier_semaphore()
    for step in range(1, peers):
        pl.semaphore_signal(barrier, inc=1, device_id=(lax.rem(s + step, peers), z), device_id_type=MESH)

    @when(z > 0)
    def _():
        pl.semaphore_signal(barrier, inc=1, device_id=(s, z - 1), device_id_type=MESH)

    @when(z < depth - 1)
    def _():
        pl.semaphore_signal(barrier, inc=1, device_id=(s, z + 1), device_id_type=MESH)

    pl.semaphore_wait(barrier, peers - 1 + jnp.where(z > 0, 1, 0) + jnp.where(z < depth - 1, 1, 0))

    halo = remote(x_hbm.at[pl.ds(rows - HALO, HALO)], ext.at[pl.ds(0, HALO)], halo_sem.at[0], halo_sem.at[1],
                  (lax.rem(s + 1, peers), z))

    @when(s < peers - 1)
    def _():
        halo.start()

    def cnt_copy(step, slot):
        return remote(cnt_ref, totals.at[slot], cnt_send.at[step], cnt_recv.at[slot],
                      (lax.rem(s + step, peers), z))

    for step in range(1, peers):
        cnt_copy(step, s).start()

    load.wait()

    @when(s == 0)
    def _():
        ext[0:HALO, :] = jnp.zeros((HALO, width), ext.dtype)

    @when(s > 0)
    def _():
        halo.wait_recv()

    block = LANES
    own_rows = pl.multiple_of(core * rows, rows)

    def conv(column):
        at = pl.ds(pl.multiple_of(column, LANES), LANES)
        taps_here = taps_ref[:, at]

        def body(r, _):
            first = pl.multiple_of(r * block, block)
            seen = ext[pl.ds(first, block + HALO), at].astype(jnp.float32)
            code = code_ref[pl.ds(first, block), :]
            lags = jnp.bitwise_and(code, taps - 1)
            total = jnp.broadcast_to(taps_here[taps : taps + 1], (block, LANES))
            for lag in range(taps):
                window = (pltpu.roll(seen, lag, 0) if lag else seen)[HALO:]
                term = jnp.broadcast_to(taps_here[lag : lag + 1], (block, LANES)) * window
                total = total + jnp.where(lags >= lag, term, 0.0)
            value = total / (1.0 + jnp.exp(-total))
            value = jnp.where(code >= taps, value, 0.0)
            feats[pl.ds(pl.multiple_of(own_rows + first, block), block), at] = value.astype(feats.dtype)
            return 0

        lax.fori_loop(0, rows // block, body, 0)

    def pair_copy(piece, row0):
        spot = feats.at[pl.ds(row0, rows), pl.ds(pl.multiple_of(piece * LANES, LANES), LANES)]
        return remote(spot, spot, pair_send.at[piece], pair_recv.at[piece], (sib, z))

    def own_piece(k):
        return feats.at[:, pl.ds(pl.multiple_of(core * half + k * LANES, LANES), LANES)]

    def up_copy(k):
        return remote(own_piece(k), got.at[z, k], up_send.at[k], got_recv.at[z, k], (s, lax.rem(z + 1, depth)))

    def down_copy(k):
        return remote(own_piece(k), got.at[z, k], down_send.at[k], got_recv.at[z, k],
                      (s, lax.rem(z + depth - 1, depth)))

    def spread(k, _):
        for side in (1 - core, core):
            piece = side * pieces + k
            conv(piece * LANES)
            pair_copy(piece, own_rows).start()
        pair_copy(core * pieces + k, own_rows).wait_recv()

        @when(z < depth - 1)
        def _():
            up_copy(k).start()

        @when(z > 0)
        def _():
            down_copy(k).start()

        return 0

    lax.fori_loop(0, pieces, spread, 0)

    def settle(k, _):
        pair_copy((1 - core) * pieces + k, own_rows).wait_recv()
        got[z, k] = feats[:, pl.ds(pl.multiple_of(core * half + k * LANES, LANES), LANES)]
        return 0

    lax.fori_loop(0, pieces, settle, 0)

    steps = pieces + 2 * pieces * (depth - 1)

    def place(i):
        later = i - pieces
        own = i < pieces
        later = jnp.where(own, 0, later)
        away = jnp.where(own, 0, later // (2 * pieces) + 1)
        k = jnp.where(own, i, lax.rem(later, 2 * pieces) // 2)
        sign = 1 - 2 * lax.rem(later, 2)
        block_at = z + sign * away
        valid = jnp.logical_and(block_at >= 0, block_at < depth)
        block_in = jnp.where(valid, block_at, 0)
        return away, k, sign, block_in, valid

    def apart(block_at):
        return lax.rem(block_at, 2) != x, block_at // 2 != y

    def fwd_copy(block_at, k, sign):
        to = lax.rem(z - sign + depth, depth)
        return remote(got.at[block_at, k], got.at[block_at, k], fwd_send.at[block_at, k], got_recv.at[block_at, k],
                      (s, to))

    def a1_copy(b, k):
        return remote(part.at[b, k, 0], from_x.at[b, k], a1_send.at[b, k], a1_recv.at[b, k], (over_x, z))

    def b1_copy(b, k):
        return remote(part.at[b, k, 1], from_y.at[b, k], b1_send.at[b, k], b1_recv.at[b, k], (over_y, z))

    def a2_copy(b, k):
        return remote(part.at[b, k, 0], sum_y.at[k], a2_send.at[b, k], a2_recv.at[k], (over_y, z))

    def b2_copy(b, k):
        return remote(part.at[b, k, 1], sum_x.at[k], b2_send.at[b, k], b2_recv.at[k], (over_x, z))

    def product(i):
        away, k, sign, b, valid = place(i)
        beyond = z - sign
        far_x, far_y = apart(b)

        @when(valid)
        def _():
            @when(away > 0)
            def _():
                fwd_copy(b, k, sign).wait_recv()

                @when(jnp.logical_and(beyond >= 0, beyond < depth))
                def _():
                    fwd_copy(b, k, sign).start()

            for side in range(2):
                part[b, k, side] = lax.dot_general(got[b, k], feats[:, side * half : (side + 1) * half],
                                                   (((0,), (0,)), ((), ())), preferred_element_type=jnp.float32)

            @when(far_x)
            def _():
                a1_copy(b, k).start()

            @when(far_y)
            def _():
                b1_copy(b, k).start()

    def combine(i):
        _, k, _, b, valid = place(i)
        far_x, far_y = apart(b)

        @when(jnp.logical_and(valid, jnp.logical_and(jnp.logical_not(far_x), far_y)))
        def _():
            a1_copy(b, k).wait_recv()
            part[b, k, 0] = part[b, k, 0] + from_x[b, k]
            a2_copy(b, k).start()

        @when(jnp.logical_and(valid, jnp.logical_and(far_x, jnp.logical_not(far_y))))
        def _():
            b1_copy(b, k).wait_recv()
            part[b, k, 1] = part[b, k, 1] + from_y[b, k]
            b2_copy(b, k).start()

    lag = 2

    def main(i, _):
        @when(i < steps)
        def _():
            product(i)

        @when(i >= lag)
        def _():
            combine(i - lag)

        return 0

    lax.fori_loop(0, steps + lag, main, 0)

    for step in range(1, peers):
        cnt_copy(step, lax.rem(s + peers - step, peers)).wait_recv()
    totals[s] = cnt_ref[...]
    token_total = jnp.sum(totals[...].astype(jnp.float32), axis=0)[0:1, :]
    scale = jnp.broadcast_to(jnp.concatenate([1.0 / token_total] * (half // LANES), axis=1), (LANES, half))

    def finish(k, _):
        at = pl.ds(pl.multiple_of(k * LANES, LANES), LANES)
        a1_copy(quad, k).wait_recv()
        a2_copy(quad, k).wait_recv()
        o_ref[at, 0:half] = (part[quad, k, 0] + from_x[quad, k] + sum_y[k]) * scale
        b1_copy(quad, k).wait_recv()
        b2_copy(quad, k).wait_recv()
        o_ref[at, half : 2 * half] = (part[quad, k, 1] + from_y[quad, k] + sum_x[k]) * scale
        return 0

    lax.fori_loop(0, pieces, finish, 0)

    @when(s < peers - 1)
    def _():
        halo.wait_send()

    for step in range(1, peers):
        cnt_copy(step, s).wait_send()

    def sent(k, _):
        for side in range(2):
            pair_copy(side * pieces + k, own_rows).wait_send()

        @when(z < depth - 1)
        def _():
            up_copy(k).wait_send()

        @when(z > 0)
        def _():
            down_copy(k).wait_send()

        return 0

    lax.fori_loop(0, pieces, sent, 0)

    def sent_late(i, _):
        away, k, sign, b, valid = place(i)
        beyond = z - sign
        far_x, far_y = apart(b)

        @when(jnp.logical_and(jnp.logical_and(valid, away > 0), jnp.logical_and(beyond >= 0, beyond < depth)))
        def _():
            fwd_copy(b, k, sign).wait_send()

        @when(jnp.logical_and(valid, far_x))
        def _():
            a1_copy(b, k).wait_send()

        @when(jnp.logical_and(valid, far_y))
        def _():
            b1_copy(b, k).wait_send()

        @when(jnp.logical_and(valid, jnp.logical_and(jnp.logical_not(far_x), far_y)))
        def _():
            a2_copy(b, k).wait_send()

        @when(jnp.logical_and(valid, jnp.logical_and(far_x, jnp.logical_not(far_y))))
        def _():
            b2_copy(b, k).wait_send()

        return 0

    lax.fori_loop(0, steps, sent_late, 0)


def fused_on_device(peers, depth, inputs, conv_weight, conv_bias, doc_start, counts):
    rows, width = inputs.shape
    taps = conv_weight.shape[0]
    half = width // 2
    pieces = half // LANES
    index = jnp.arange(rows, dtype=jnp.int32)
    reach = jnp.minimum(lax.axis_index("seq") * rows + index - doc_start, taps - 1)
    code = reach + jnp.where(index < counts[0], taps, 0)
    code = jnp.broadcast_to(code[:, None], (rows, LANES))
    cnt = jnp.broadcast_to(counts[0], (8, LANES))
    taps_bias = jnp.concatenate([conv_weight, conv_bias[None]], axis=0).astype(jnp.float32)
    vmem = pl.BlockSpec(memory_space=pltpu.VMEM)
    dma = lambda *shape: pltpu.SemaphoreType.DMA(shape)
    f32 = jnp.float32
    grid = (depth, pieces)
    return pl.pallas_call(
        functools.partial(gram_kernel, peers, depth, taps),
        out_shape=jax.ShapeDtypeStruct((half, width), f32),
        in_specs=[pl.BlockSpec(memory_space=pl.ANY), vmem, vmem, vmem],
        out_specs=vmem,
        scratch_shapes=[
            pltpu.VMEM((rows + HALO, width), inputs.dtype),
            pltpu.VMEM((2 * rows, width), inputs.dtype),
            pltpu.VMEM((depth, pieces, 2 * rows, LANES), inputs.dtype),
            pltpu.VMEM((depth, pieces, 2, LANES, half), f32),
            pltpu.VMEM((depth, pieces, LANES, half), f32),
            pltpu.VMEM((depth, pieces, LANES, half), f32),
            pltpu.VMEM((pieces, LANES, half), f32),
            pltpu.VMEM((pieces, LANES, half), f32),
            pltpu.VMEM((peers, 8, LANES), jnp.int32),
            pltpu.SemaphoreType.DMA, dma(2), dma(peers), dma(peers), dma(2 * pieces), dma(2 * pieces),
            dma(pieces), dma(pieces), dma(*grid), dma(*grid),
            dma(*grid), dma(*grid), dma(*grid), dma(*grid), dma(*grid), dma(pieces), dma(*grid), dma(pieces),
        ],
        compiler_params=pltpu.CompilerParams(collective_id=0, has_side_effects=True,
                                             vmem_limit_bytes=60 * 1024 * 1024),
        name="gram",
    )(inputs, taps_bias, code, cnt)


def passed_along(x, axis, by):
    peers = lax.axis_size(axis)
    pairs = [(i, i + by) for i in range(peers) if 0 <= i + by < peers]
    return lax.ppermute(x, axis, pairs)


def causal_conv(extended, weights, bias, position, doc_start, length):
    kernel_len = weights.shape[0]
    summed = jnp.zeros((length, weights.shape[1]), jnp.float32) + bias.astype(jnp.float32)
    for lag in range(kernel_len):
        window = extended[kernel_len - 1 - lag : kernel_len - 1 - lag + length].astype(jnp.float32)
        usable = position - lag >= doc_start
        summed = summed + jnp.where(usable[:, None], weights[lag].astype(jnp.float32) * window, 0.0)
    return jax.nn.silu(summed).astype(jnp.bfloat16)


def on_device(inputs, conv_weight, conv_bias, doc_start, counts):
    row_count = inputs.shape[0]
    kernel_len = conv_weight.shape[0]
    position = lax.axis_index("seq") * row_count + jnp.arange(row_count, dtype=jnp.int32)
    counted = jnp.arange(row_count, dtype=jnp.int32) < counts[0]
    token_total = lax.psum(counts.astype(jnp.float32)[0], "seq")
    prior = passed_along(inputs[row_count - (kernel_len - 1) :], "seq", 1)
    extended = jnp.concatenate([prior, inputs], axis=0)
    own_feats = causal_conv(extended, conv_weight, conv_bias, position, doc_start, row_count)
    kept = jnp.where(counted[:, None], own_feats, jnp.zeros_like(own_feats))
    whole = lax.all_gather(own_feats, "mp", axis=1, tiled=True)
    summed = lax.psum_scatter(
        lax.dot_general(whole, kept, (((0,), (0,)), ((), ())), preferred_element_type=jnp.float32),
        "seq",
        scatter_dimension=0,
        tiled=True,
    )
    return summed / token_total


def solution(mesh):
    placed = (P("seq", "mp"), P(None, "mp"), P("mp"), P("seq"), P("seq"))
    peers, depth = mesh.shape["seq"], mesh.shape["mp"]
    fits = peers == 2 * depth and peers == 2**3
    body = functools.partial(fused_on_device, peers, depth) if fits else on_device
    return jax.shard_map(body, mesh=mesh, in_specs=placed, out_specs=P("seq", "mp"), check_vma=False)
```

profile of v0, /device:TPU:6, one launch (start us, length us, event | category | flops | bytes accessed | tf_op | source)
XLA Modules:
  0.0 176.3 jit_solution(2934907971771485169)
XLA Ops:
  0.7 0.7 select_add_fusion
  1.3 0.7 broadcast_in_dim.20
  2.0 0.6 broadcast_in_dim.24.cnt_ref
  2.6 1.3 maximum_convert_fusion.taps_ref
  3.9 1.0 broadcast_in_dim.23.code_ref
  4.9 168.2 %gram.1 = f32[512,1024]{1,0:T(8,128)} custom-call(bf16[1024,1024]{1,0:T(8,128)(2,1)} %x_hbm.1, f32[5,1024]{1,0:T(8,128)} %maximum_convert_fusion.taps_ref, s32[1024,128]{1,0:T(8,128)} %broadcast_in_dim.23.code_ref, s32[8,128]{1,0:T(8,128)} %broadcast_in_dim.24.cnt_ref), custom_call_target="tpu_custom_call" | custom-call | tf_op jit(solution)/shard_map/gram/pallas_call | solution.py:319
  173.2 3.2 %copy.8 = f32[512,1024]{1,0:T(8,128)} copy(f32[512,1024]{1,0:T(8,128)} %gram.1) | data formatting | bytes 4194304
where the time goes:
time: 177 us; the launch traced here: 176 us
  Pallas kernels  168 us (95%)
  local copies, waits for them, and re-layouts  5.43 us (3%)
  other arithmetic  2 us (1%)
    pallas_call x1, Pallas kernels, fused_on_device(): pl.pallas_call(functools.partial(gram_kernel, peers, depth, taps), out_sh...  168 us

commit v1 on v0

v1 whole, which is shorter than its diff:
```python
import functools

import jax
import jax.numpy as jnp
from jax import lax
from jax.experimental import pallas as pl
from jax.experimental.pallas import tpu as pltpu
from jax.sharding import PartitionSpec as P

MESH = pl.DeviceIdType.MESH
LANES = 128
HALO = 16


def when(cond):
    return pl.when(cond)


TINY = 1e-30
STEPS = 32767.0


class Group:
    def __init__(self, *copies):
        self.copies = copies

    def start(self):
        for copy in self.copies:
            copy.start()

    def wait_send(self):
        for copy in self.copies:
            copy.wait_send()

    def wait_recv(self):
        for copy in self.copies:
            copy.wait_recv()


def gram_kernel(peers, depth, taps, near, relayed, x_hbm, taps_ref, bias_ref, doc_ref, counts_ref, o_ref, ext, feats, got, part,
                from_x, from_y, sum_y, sum_x, rim, rpart, rfrom_x, rfrom_y, rsum_y, rsum_x, ready, readyu, landed, landedu, totals,
                lag_ref, cnt_ref, bias_rows, code, unit, from_xu, from_yu, sum_yu, sum_xu, rcode, runit, rfrom_xu, rfrom_yu, rsum_yu, rsum_xu,
                load_sem, halo_sem, cnt_send, cnt_recv, pair_send, pair_recv,
                up_send, down_send, fwd_send, got_recv,
                a1_send, a1_recv, b1_send, b1_recv, a2_send, a2_recv, b2_send, b2_recv,
                share_send, share_recv, ra1_send, ra1_recv, rb1_send, rb1_recv,
                ra2_send, ra2_recv, rb2_send, rb2_recv, land_send, land_recv):
    s, z = lax.axis_index("seq"), lax.axis_index("mp")
    core, x, y = lax.rem(s, 2), lax.rem(s // 2, 2), s // 4
    sib, over_x, over_y = s + 1 - 2 * core, s + 2 - 4 * x, s + 4 - 8 * y
    quad = s // 2
    rows, width = x_hbm.shape
    half = width // 2
    pieces = half // LANES
    on_rim = jnp.logical_or(z == 0, z == depth - 1)
    inside = jnp.logical_not(on_rim)
    orient = jnp.where(z < depth // 2, 1, -1)
    outer = jnp.where(z < depth // 2, 0, depth - 1)

    def remote(src, dst, send, recv, to):
        return pltpu.make_async_remote_copy(src_ref=src, dst_ref=dst, send_sem=send, recv_sem=recv,
                                            device_id=to, device_id_type=MESH)

    def both(*conds):
        return functools.reduce(jnp.logical_and, conds)

    def either(*conds):
        return functools.reduce(jnp.logical_or, conds)

    load = pltpu.make_async_copy(x_hbm, ext.at[pl.ds(HALO, rows)], load_sem)
    load.start()

    barrier = pltpu.get_barrier_semaphore()
    for step in range(1, peers):
        pl.semaphore_signal(barrier, inc=1, device_id=(lax.rem(s + step, peers), z), device_id_type=MESH)

    @when(z > 0)
    def _():
        pl.semaphore_signal(barrier, inc=1, device_id=(s, z - 1), device_id_type=MESH)

    @when(z < depth - 1)
    def _():
        pl.semaphore_signal(barrier, inc=1, device_id=(s, z + 1), device_id_type=MESH)

    bias_rows[...] = bias_ref[...].astype(jnp.float32)
    cnt_ref[...] = jnp.broadcast_to(counts_ref[0], cnt_ref.shape)
    block = LANES

    def mark_block(r, _):
        first = pl.multiple_of(r * block, block)
        within = first + lax.broadcasted_iota(jnp.int32, (block, LANES), 0)
        start = jnp.transpose(jnp.broadcast_to(doc_ref[pl.ds(r, 1), :], (block, LANES)))
        reach = jnp.minimum(s * rows + within - start, taps - 1)
        lag_ref[pl.ds(first, block), :] = reach + jnp.where(within < counts_ref[0], taps, 0)
        return 0

    lax.fori_loop(0, rows // block, mark_block, 0)

    load.wait()
    pl.semaphore_wait(barrier, peers - 1 + jnp.where(z > 0, 1, 0) + jnp.where(z < depth - 1, 1, 0))

    halo = remote(ext.at[pl.ds(rows, HALO)], ext.at[pl.ds(0, HALO)], halo_sem.at[0], halo_sem.at[1],
                  (lax.rem(s + 1, peers), z))

    @when(s < peers - 1)
    def _():
        halo.start()

    def cnt_copy(step, slot):
        return remote(cnt_ref, totals.at[slot], cnt_send.at[step], cnt_recv.at[slot],
                      (lax.rem(s + step, peers), z))

    for step in range(1, peers):
        cnt_copy(step, s).start()

    own_rows = pl.multiple_of(core * rows, rows)

    def conv(column, low, high):
        at = pl.ds(pl.multiple_of(column, LANES), LANES)
        taps_here = taps_ref[:, at].astype(jnp.float32)
        bias_here = bias_rows[pl.ds(column // LANES, 1), :]

        def body(r, _):
            first = pl.multiple_of(r * block, block)
            seen = ext[pl.ds(first, block + HALO), at].astype(jnp.float32)
            mark = lag_ref[pl.ds(first, block), :]
            lags = jnp.bitwise_and(mark, taps - 1)
            total = jnp.broadcast_to(bias_here, (block, LANES))
            for lag_ in range(taps):
                window = (pltpu.roll(seen, lag_, 0) if lag_ else seen)[HALO:]
                term = jnp.broadcast_to(taps_here[lag_ : lag_ + 1], (block, LANES)) * window
                total = total + jnp.where(lags >= lag_, term, 0.0)
            value = total / (1.0 + jnp.exp(-total))
            value = jnp.where(mark >= taps, value, 0.0)
            feats[pl.ds(pl.multiple_of(own_rows + first, block), block), at] = value.astype(feats.dtype)
            return 0

        lax.fori_loop(low, high, body, 0)

    def pair_copy(piece, row0):
        spot = feats.at[pl.ds(row0, rows), pl.ds(pl.multiple_of(piece * LANES, LANES), LANES)]
        return remote(spot, spot, pair_send.at[piece], pair_recv.at[piece], (sib, z))

    def own_columns(k):
        return pl.ds(pl.multiple_of(core * half + k * LANES, LANES), LANES)

    def tokens(j):
        return pl.ds(pl.multiple_of(j * rows, rows), rows)

    def up_copy(k, j):
        return remote(feats.at[tokens(j), own_columns(k)], got.at[z, k, tokens(j)], up_send.at[k, j],
                      got_recv.at[z, k, j], (s, lax.rem(z + 1, depth)))

    def down_copy(k, j):
        return remote(feats.at[tokens(j), own_columns(k)], got.at[z, k, tokens(j)], down_send.at[k, j],
                      got_recv.at[z, k, j], (s, lax.rem(z + depth - 1, depth)))

    def goes_up(k):
        return either(z < depth - 2, both(z == depth - 2, k >= near))

    def goes_down(k):
        return either(z > 1, both(z == 1, k >= near))

    blocks = rows // block
    for side in (1 - core, core):
        conv(side * half, 1, blocks)

    @when(s == 0)
    def _():
        ext[0:HALO, :] = jnp.zeros((HALO, width), ext.dtype)

    @when(s > 0)
    def _():
        halo.wait_recv()

    def spread(k, _):
        def make(side):
            piece = side * pieces + k
            conv(piece * LANES, 0, jnp.where(k == 0, 1, blocks))
            pair_copy(piece, own_rows).start()


        def send(j):
            @when(goes_up(k))
            def _():
                up_copy(k, j).start()

            @when(goes_down(k))
            def _():
                down_copy(k, j).start()

        make(1 - core)
        make(core)
        send(core)
        pair_copy(core * pieces + k, own_rows).wait_recv()
        send(1 - core)
        return 0

    lax.fori_loop(0, pieces, spread, 0)

    def settle(k, _):
        pair_copy((1 - core) * pieces + k, own_rows).wait_recv()
        got[z, k] = feats[:, own_columns(k)]
        return 0

    lax.fori_loop(0, pieces, settle, 0)

    steps = pieces + 2 * pieces * (depth - 1)

    def quota(span):
        return jnp.where(span == depth - 1, relayed, near)

    def place(i):
        later = i - pieces
        own = i < pieces
        later = jnp.where(own, 0, later)
        away = jnp.where(own, 0, later // (2 * pieces) + 1)
        k = jnp.where(own, i, lax.rem(later, 2 * pieces) // 2)
        second = both(jnp.logical_not(own), lax.rem(later, 2) == 1)
        sign = jnp.where(second, -orient, orient)
        block_at = z + sign * away
        within = both(block_at >= 0, block_at < depth)
        block_in = jnp.where(within, block_at, 0)
        valid = both(within, either(own, inside, k >= quota(away)))
        relay = both(inside, away == 2, second)
        return away, k, sign, block_in, valid, second, relay

    def onward(away, k, sign, valid):
        beyond = z - sign
        deep = both(beyond > 0, beyond < depth - 1)
        edge = either(beyond == 0, beyond == depth - 1)
        return both(valid, away > 0, either(deep, both(edge, k >= quota(away + 1))))

    def apart(block_at):
        return lax.rem(block_at, 2) != x, block_at // 2 != y

    def fwd_copy(block_at, k, j, sign):
        to = lax.rem(z - sign + depth, depth)
        return remote(got.at[block_at, k, tokens(j)], got.at[block_at, k, tokens(j)], fwd_send.at[block_at, k, j],
                      got_recv.at[block_at, k, j], (s, to))

    def coded(src, srcu, dst, dstu, send, recv, to):
        return Group(remote(src, dst, send.at[0], recv.at[0], to), remote(srcu, dstu, send.at[1], recv.at[1], to))

    def a1_copy(b, k):
        return coded(code.at[b, k, 0], unit.at[b, k, 0], from_x.at[b, k], from_xu.at[b, k],
                     a1_send.at[b, k], a1_recv.at[b, k], (over_x, z))

    def b1_copy(b, k):
        return coded(code.at[b, k, 1], unit.at[b, k, 1], from_y.at[b, k], from_yu.at[b, k],
                     b1_send.at[b, k], b1_recv.at[b, k], (over_y, z))

    def a2_copy(b, k):
        return coded(code.at[b, k, 0], unit.at[b, k, 0], sum_y.at[k], sum_yu.at[k],
                     a2_send.at[k], a2_recv.at[k], (over_y, z))

    def b2_copy(b, k):
        return coded(code.at[b, k, 1], unit.at[b, k, 1], sum_x.at[k], sum_xu.at[k],
                     b2_send.at[k], b2_recv.at[k], (over_x, z))

    def share_copy(k):
        return remote(got.at[outer, k], rim.at[:, own_columns(k)], share_send.at[k], share_recv.at[k], (sib, z))

    def ra1_copy(j, k):
        return coded(rcode.at[j, k, 0], runit.at[j, k, 0], rfrom_x.at[j, k], rfrom_xu.at[j, k],
                     ra1_send.at[j, k], ra1_recv.at[j, k], (over_x, z))

    def rb1_copy(j, k):
        return coded(rcode.at[j, k, 1], runit.at[j, k, 1], rfrom_y.at[j, k], rfrom_yu.at[j, k],
                     rb1_send.at[j, k], rb1_recv.at[j, k], (over_y, z))

    def ra2_copy(j, k):
        return coded(rcode.at[j, k, 0], runit.at[j, k, 0], rsum_y.at[k], rsum_yu.at[k],
                     ra2_send.at[k], ra2_recv.at[k], (over_y, z))

    def rb2_copy(j, k):
        return coded(rcode.at[j, k, 1], runit.at[j, k, 1], rsum_x.at[k], rsum_xu.at[k],
                     rb2_send.at[k], rb2_recv.at[k], (over_x, z))

    def land_copy(k):
        return coded(ready.at[k], readyu.at[k], landed.at[k], landedu.at[k],
                     land_send.at[k], land_recv.at[k], (s, outer))

    def multiply(left, right):
        return lax.dot_general(left, right, (((0,), (0,)), ((), ())), preferred_element_type=jnp.float32)

    def encode(value, code_at, unit_at):
        top = jnp.maximum(jnp.max(jnp.abs(value), axis=0, keepdims=True), TINY)
        code_at[...] = jnp.round(value * (STEPS / top)).astype(jnp.int32).astype(jnp.int16)
        unit_at[...] = top * (1.0 / STEPS)

    def decode(codes, units):
        return codes.astype(jnp.int32).astype(jnp.float32) * units

    def stage(value, away_from_here, part_at, code_at, unit_at):
        @when(away_from_here)
        def _():
            encode(value, code_at, unit_at)

        @when(jnp.logical_not(away_from_here))
        def _():
            part_at[...] = value

    def relayed_block(j):
        return jnp.where(inside, z + orient * j, 0)

    def gathered(i):
        return both(inside, i == 3 * pieces - 1)

    def relay_product(j, k):
        b = relayed_block(j)
        far_x, far_y = apart(b)
        for side in range(2):
            stage(multiply(got[b, k], rim[:, side * half : (side + 1) * half]), (far_x, far_y)[side],
                  rpart.at[j, k, side], rcode.at[j, k, side], runit.at[j, k, side])

        @when(far_x)
        def _():
            ra1_copy(j, k).start()

        @when(far_y)
        def _():
            rb1_copy(j, k).start()

    def relay_combine(j, k):
        far_x, far_y = apart(relayed_block(j))

        @when(both(jnp.logical_not(far_x), far_y))
        def _():
            ra1_copy(j, k).wait_recv()
            encode(rpart[j, k, 0] + decode(rfrom_x[j, k], rfrom_xu[j, k]), rcode.at[j, k, 0], runit.at[j, k, 0])
            ra2_copy(j, k).start()

        @when(both(far_x, jnp.logical_not(far_y)))
        def _():
            rb1_copy(j, k).wait_recv()
            encode(rpart[j, k, 1] + decode(rfrom_y[j, k], rfrom_yu[j, k]), rcode.at[j, k, 1], runit.at[j, k, 1])
            rb2_copy(j, k).start()

    def product(i):
        away, k, sign, b, valid, second, relay = place(i)
        far_x, far_y = apart(b)
        passes = onward(away, k, sign, valid)

        @when(valid)
        def _():
            @when(away > 0)
            def _():
                for j in (core, 1 - core):
                    fwd_copy(b, k, j, sign).wait_recv()

                    @when(passes)
                    def _():
                        fwd_copy(b, k, j, sign).start()

                @when(both(inside, b == outer))
                def _():
                    share_copy(k).start()
                    rim[:, own_columns(k)] = got[b, k]

            for side in range(2):
                stage(multiply(got[b, k], feats[:, side * half : (side + 1) * half]), (far_x, far_y)[side],
                      part.at[b, k, side], code.at[b, k, side], unit.at[b, k, side])

            @when(far_x)
            def _():
                a1_copy(b, k).start()

            @when(far_y)
            def _():
                b1_copy(b, k).start()

        @when(gathered(i))
        def _():
            for p in range(pieces):
                share_copy(p).wait_recv()

            lax.fori_loop(0, near * (depth - 2), lambda m, _: (relay_product(m // near, lax.rem(m, near)), 0)[1], 0)

        @when(both(relay, k < relayed))
        def _():
            relay_product(depth - 2, k)

    home = (quad - z) * orient

    def hand_over(k):
        ra1_copy(home, k).wait_recv()
        ra2_copy(home, k).wait_recv()
        encode(rpart[home, k, 0] + decode(rfrom_x[home, k], rfrom_xu[home, k]) + decode(rsum_y[k], rsum_yu[k]),
               ready.at[k, :, 0:half], readyu.at[k, :, 0:half])
        rb1_copy(home, k).wait_recv()
        rb2_copy(home, k).wait_recv()
        encode(rpart[home, k, 1] + decode(rfrom_y[home, k], rfrom_yu[home, k]) + decode(rsum_x[k], rsum_xu[k]),
               ready.at[k, :, half : 2 * half], readyu.at[k, :, half : 2 * half])
        land_copy(k).start()

    def hand_over_early(i):
        @when(both(inside, quad != outer, home < depth - 2, i == base + 2))
        def _():
            lax.fori_loop(0, near, lambda k, _: (hand_over(k), 0)[1], 0)

        for k in range(relayed):
            @when(both(inside, home == depth - 2, i == base + 4 + 3 * k))
            def _():
                hand_over(k)

    def combine(i):
        _, k, _, b, valid, _, relay = place(i)
        far_x, far_y = apart(b)

        @when(both(valid, jnp.logical_not(far_x), far_y))
        def _():
            a1_copy(b, k).wait_recv()
            encode(part[b, k, 0] + decode(from_x[b, k], from_xu[b, k]), code.at[b, k, 0], unit.at[b, k, 0])
            a2_copy(b, k).start()

        @when(both(valid, far_x, jnp.logical_not(far_y)))
        def _():
            b1_copy(b, k).wait_recv()
            encode(part[b, k, 1] + decode(from_y[b, k], from_yu[b, k]), code.at[b, k, 1], unit.at[b, k, 1])
            b2_copy(b, k).start()

        @when(gathered(i))
        def _():
            lax.fori_loop(0, near * (depth - 2), lambda m, _: (relay_combine(m // near, lax.rem(m, near)), 0)[1], 0)

        @when(both(relay, k < relayed))
        def _():
            relay_combine(depth - 2, k)

    base = 3 * pieces

    def sent(k, _):
        for side in range(2):
            pair_copy(side * pieces + k, own_rows).wait_send()

        for j in range(2):
            @when(goes_up(k))
            def _():
                up_copy(k, j).wait_send()

            @when(goes_down(k))
            def _():
                down_copy(k, j).wait_send()

        @when(inside)
        def _():
            share_copy(k).wait_send()

        return 0

    def sent_late(i, _):
        away, k, sign, b, valid, _, relay = place(i)
        far_x, far_y = apart(b)

        @when(onward(away, k, sign, valid))
        def _():
            for j in range(2):
                fwd_copy(b, k, j, sign).wait_send()

        @when(both(valid, far_x))
        def _():
            a1_copy(b, k).wait_send()

        @when(both(valid, far_y))
        def _():
            b1_copy(b, k).wait_send()

        @when(both(valid, jnp.logical_not(far_x), far_y))
        def _():
            a2_copy(b, k).wait_send()

        @when(both(valid, far_x, jnp.logical_not(far_y)))
        def _():
            b2_copy(b, k).wait_send()

        return 0

    def main(i, _):
        @when(both(i >= base, lax.rem(i, 2) == 0))
        def _():
            combine(i - 2)
            combine(i - 1)

        hand_over_early(i)

        @when(both(i >= base, i < steps))
        def _():
            sent_late(i - base, 0)

        @when(both(i >= base, i < base + pieces))
        def _():
            sent(i - base, 0)

        @when(i < steps)
        def _():
            product(i)

        @when(both(i > pieces, i < base, lax.rem(i, 2) == 1))
        def _():
            combine((i - pieces) // 2)

            @when(i > pieces + 1)
            def _():
                combine(i - 3)
                combine(i - 2)

        return 0

    lax.fori_loop(0, steps + 1, main, 0)

    for step in range(1, peers):
        cnt_copy(step, lax.rem(s + peers - step, peers)).wait_recv()
    totals[s] = cnt_ref[...]
    token_total = jnp.sum(totals[...].astype(jnp.float32), axis=0)[0:1, :]
    scale = jnp.broadcast_to(jnp.concatenate([1.0 / token_total] * (half // LANES), axis=1), (LANES, half))

    def local(k):
        return either(inside, k >= quota(jnp.abs(quad - z)), quad == z)

    def finish(k, _):
        at = pl.ds(pl.multiple_of(k * LANES, LANES), LANES)

        @when(local(k))
        def _():
            a1_copy(quad, k).wait_recv()
            a2_copy(quad, k).wait_recv()
            o_ref[at, 0:half] = (part[quad, k, 0] + decode(from_x[quad, k], from_xu[quad, k])
                                 + decode(sum_y[k], sum_yu[k])) * scale
            b1_copy(quad, k).wait_recv()
            b2_copy(quad, k).wait_recv()
            o_ref[at, half : 2 * half] = (part[quad, k, 1] + decode(from_y[quad, k], from_yu[quad, k])
                                          + decode(sum_x[k], sum_xu[k])) * scale

        return 0

    lax.fori_loop(0, pieces, finish, 0)

    def take(k, _):
        at = pl.ds(pl.multiple_of(k * LANES, LANES), LANES)

        @when(both(on_rim, quad != z, k < quota(jnp.abs(quad - z))))
        def _():
            land_copy(k).wait_recv()
            for side in range(2):
                cols = slice(side * half, (side + 1) * half)
                o_ref[at, cols] = decode(landed[k, :, cols], landedu[k, :, cols]) * scale

        return 0

    lax.fori_loop(0, relayed, take, 0)

    @when(s < peers - 1)
    def _():
        halo.wait_send()

    for step in range(1, peers):
        cnt_copy(step, s).wait_send()

    lax.fori_loop(steps - base, steps, sent_late, 0)

    def sent_relayed(m, _):
        j, k = m // relayed, lax.rem(m, relayed)
        far_x, far_y = apart(relayed_block(j))
        live = both(inside, k < quota(j + 1))

        @when(both(live, far_x))
        def _():
            ra1_copy(j, k).wait_send()

        @when(both(live, far_y))
        def _():
            rb1_copy(j, k).wait_send()

        @when(both(live, jnp.logical_not(far_x), far_y))
        def _():
            ra2_copy(j, k).wait_send()

        @when(both(live, far_x, jnp.logical_not(far_y)))
        def _():
            rb2_copy(j, k).wait_send()

        @when(both(live, j == home))
        def _():
            land_copy(k).wait_send()

        return 0

    lax.fori_loop(0, relayed * (depth - 1), sent_relayed, 0)


def fused_on_device(peers, depth, inputs, conv_weight, conv_bias, doc_start, counts):
    rows, width = inputs.shape
    taps = conv_weight.shape[0]
    half = width // 2
    pieces = half // LANES
    relayed = pieces // 2
    vmem = pl.BlockSpec(memory_space=pltpu.VMEM)
    dma = lambda *shape: pltpu.SemaphoreType.DMA(shape)
    f32, i16 = jnp.float32, jnp.int16
    grid = (depth, pieces)
    outs = (depth - 1, relayed)
    return pl.pallas_call(
        functools.partial(gram_kernel, peers, depth, taps, 1, relayed),
        out_shape=jax.ShapeDtypeStruct((half, width), f32),
        in_specs=[pl.BlockSpec(memory_space=pl.ANY), vmem, vmem, vmem, pl.BlockSpec(memory_space=pltpu.SMEM)],
        out_specs=vmem,
        scratch_shapes=[
            pltpu.VMEM((rows + HALO, width), inputs.dtype),
            pltpu.VMEM((2 * rows, width), inputs.dtype),
            pltpu.VMEM((depth, pieces, 2 * rows, LANES), inputs.dtype),
            pltpu.VMEM((depth, pieces, 2, LANES, half), f32),
            pltpu.VMEM((depth, pieces, LANES, half), i16),
            pltpu.VMEM((depth, pieces, LANES, half), i16),
            pltpu.VMEM((pieces, LANES, half), i16),
            pltpu.VMEM((pieces, LANES, half), i16),
            pltpu.VMEM((2 * rows, width), inputs.dtype),
            pltpu.VMEM((*outs, 2, LANES, half), f32),
            pltpu.VMEM((*outs, LANES, half), i16),
            pltpu.VMEM((*outs, LANES, half), i16),
            pltpu.VMEM((relayed, LANES, half), i16),
            pltpu.VMEM((relayed, LANES, half), i16),
            pltpu.VMEM((relayed, LANES, width), i16),
            pltpu.VMEM((relayed, 1, width), f32),
            pltpu.VMEM((relayed, LANES, width), i16),
            pltpu.VMEM((relayed, 1, width), f32),
            pltpu.VMEM((peers, 8, LANES), jnp.int32),
            pltpu.VMEM((rows, LANES), jnp.int32),
            pltpu.VMEM((8, LANES), jnp.int32),
            pltpu.VMEM((width // LANES, LANES), f32),
            pltpu.VMEM((*grid, 2, LANES, half), i16),
            pltpu.VMEM((*grid, 2, 1, half), f32),
            pltpu.VMEM((*grid, 1, half), f32),
            pltpu.VMEM((*grid, 1, half), f32),
            pltpu.VMEM((pieces, 1, half), f32),
            pltpu.VMEM((pieces, 1, half), f32),
            pltpu.VMEM((*outs, 2, LANES, half), i16),
            pltpu.VMEM((*outs, 2, 1, half), f32),
            pltpu.VMEM((*outs, 1, half), f32),
            pltpu.VMEM((*outs, 1, half), f32),
            pltpu.VMEM((relayed, 1, half), f32),
            pltpu.VMEM((relayed, 1, half), f32),
            pltpu.SemaphoreType.DMA, dma(2), dma(peers), dma(peers), dma(2 * pieces), dma(2 * pieces),
            dma(pieces, 2), dma(pieces, 2), dma(*grid, 2), dma(*grid, 2),
            dma(*grid, 2), dma(*grid, 2), dma(*grid, 2), dma(*grid, 2),
            dma(pieces, 2), dma(pieces, 2), dma(pieces, 2), dma(pieces, 2),
            dma(pieces), dma(pieces), dma(*outs, 2), dma(*outs, 2), dma(*outs, 2), dma(*outs, 2),
            dma(relayed, 2), dma(relayed, 2), dma(relayed, 2), dma(relayed, 2), dma(relayed, 2), dma(relayed, 2),
        ],
        compiler_params=pltpu.CompilerParams(collective_id=0, has_side_effects=True,
                                             vmem_limit_bytes=63 * 1024 * 1024),
        name="gram",
    )(inputs, conv_weight, conv_bias.reshape(width // LANES, LANES), doc_start.reshape(rows // LANES, LANES), counts)


def passed_along(x, axis, by):
    peers = lax.axis_size(axis)
    pairs = [(i, i + by) for i in range(peers) if 0 <= i + by < peers]
    return lax.ppermute(x, axis, pairs)


def causal_conv(extended, weights, bias, position, doc_start, length):
    kernel_len = weights.shape[0]
    summed = jnp.zeros((length, weights.shape[1]), jnp.float32) + bias.astype(jnp.float32)
    for lag in range(kernel_len):
        window = extended[kernel_len - 1 - lag : kernel_len - 1 - lag + length].astype(jnp.float32)
        usable = position - lag >= doc_start
        summed = summed + jnp.where(usable[:, None], weights[lag].astype(jnp.float32) * window, 0.0)
    return jax.nn.silu(summed).astype(jnp.bfloat16)


def on_device(inputs, conv_weight, conv_bias, doc_start, counts):
    row_count = inputs.shape[0]
    kernel_len = conv_weight.shape[0]
    position = lax.axis_index("seq") * row_count + jnp.arange(row_count, dtype=jnp.int32)
    counted = jnp.arange(row_count, dtype=jnp.int32) < counts[0]
    token_total = lax.psum(counts.astype(jnp.float32)[0], "seq")
    prior = passed_along(inputs[row_count - (kernel_len - 1) :], "seq", 1)
    extended = jnp.concatenate([prior, inputs], axis=0)
    own_feats = causal_conv(extended, conv_weight, conv_bias, position, doc_start, row_count)
    kept = jnp.where(counted[:, None], own_feats, jnp.zeros_like(own_feats))
    whole = lax.all_gather(own_feats, "mp", axis=1, tiled=True)
    summed = lax.psum_scatter(
        lax.dot_general(whole, kept, (((0,), (0,)), ((), ())), preferred_element_type=jnp.float32),
        "seq",
        scatter_dimension=0,
        tiled=True,
    )
    return summed / token_total


def solution(mesh):
    placed = (P("seq", "mp"), P(None, "mp"), P("mp"), P("seq"), P("seq"))
    peers, depth = mesh.shape["seq"], mesh.shape["mp"]
    fits = peers == 2 * depth and depth == 2**2
    body = functools.partial(fused_on_device, peers, depth) if fits else on_device
    return jax.shard_map(body, mesh=mesh, in_specs=placed, out_specs=P("seq", "mp"), check_vma=False)
```

time: 177 us -> 126 us (0.71)
  Pallas kernels: 168 us -> 122 us
  local copies, waits for them, and re-layouts: 5.43 us -> 3.16 us
  other arithmetic: 2 us -> 0 us
    pallas_call x1, Pallas kernels: 168 us -> 122 us  [fused_on_device(): pl.pallas_call(functools.partial(gram_kernel, peers, depth, taps, 1, rela...]
    broadcast_in_dim x3 -> x0, local copies, waits for them, and re-layouts: 2.27 us -> none  [the longest x1 0.99 us: fused_on_device(): code = jnp.broadcast_to(code[:, None], (rows, LANES))]
where the time goes in v1:
time: 126 us
  Pallas kernels  122 us (97%)
  local copies, waits for them, and re-layouts  3.16 us (3%)
    pallas_call x1, Pallas kernels, fused_on_device(): pl.pallas_call(functools.partial(gram_kernel, peers, depth, taps, 1, rela...  122 us
    unnamed x1, local copies, waits for them, and re-layouts  3.16 us

profile of v1, /device:TPU:6, one launch (start us, length us, event | category | flops | bytes accessed | tf_op | source)
XLA Modules:
  0.0 126.1 jit_solution(6101450424977038200)
XLA Ops:
  0.7 122.3 %gram.1 = f32[512,1024]{1,0:T(8,128)} custom-call(bf16[1024,1024]{1,0:T(8,128)(2,1)} %x_hbm.1, bf16[4,1024]{1,0:T(4,128)(2,1)} %taps_ref.1, bf16[8,128]{1,0:T(8,128)(2,1)} %bitcast.3, s32[8,128]{1,0:T(8,128)} %bitcast.2, s32[1]{0:T(128)S(6)} %copy.7.counts_ref), custom_call_target="tpu_custom_call" | custom-call | tf_op jit(solution)/shard_map/gram/pallas_call | solution.py:603
  122.9 3.2 %copy.8 = f32[512,1024]{1,0:T(8,128)} copy(f32[512,1024]{1,0:T(8,128)} %gram.1) | data formatting | bytes 4194304

commit v2 on v1

--- a/solution.py
+++ b/solution.py
@@ -243,12 +243,12 @@
         return Group(remote(src, dst, send.at[0], recv.at[0], to), remote(srcu, dstu, send.at[1], recv.at[1], to))
 
     def a1_copy(b, k):
-        return coded(code.at[b, k, 0], unit.at[b, k, 0], from_x.at[b, k], from_xu.at[b, k],
-                     a1_send.at[b, k], a1_recv.at[b, k], (over_x, z))
+        return coded(code.at[b, k, 0], unit.at[b, k, 0], from_x.at[b // 2, k], from_xu.at[b // 2, k],
+                     a1_send.at[b // 2, k], a1_recv.at[b // 2, k], (over_x, z))
 
     def b1_copy(b, k):
-        return coded(code.at[b, k, 1], unit.at[b, k, 1], from_y.at[b, k], from_yu.at[b, k],
-                     b1_send.at[b, k], b1_recv.at[b, k], (over_y, z))
+        return coded(code.at[b, k, 1], unit.at[b, k, 1], from_y.at[b % 2, k], from_yu.at[b % 2, k],
+                     b1_send.at[b % 2, k], b1_recv.at[b % 2, k], (over_y, z))
 
     def a2_copy(b, k):
         return coded(code.at[b, k, 0], unit.at[b, k, 0], sum_y.at[k], sum_yu.at[k],
@@ -262,12 +262,12 @@
         return remote(got.at[outer, k], rim.at[:, own_columns(k)], share_send.at[k], share_recv.at[k], (sib, z))
 
     def ra1_copy(j, k):
-        return coded(rcode.at[j, k, 0], runit.at[j, k, 0], rfrom_x.at[j, k], rfrom_xu.at[j, k],
-                     ra1_send.at[j, k], ra1_recv.at[j, k], (over_x, z))
+        return coded(rcode.at[j, k, 0], runit.at[j, k, 0], rfrom_x.at[relayed_block(j) // 2, k], rfrom_xu.at[relayed_block(j) // 2, k],
+                     ra1_send.at[relayed_block(j) // 2, k], ra1_recv.at[relayed_block(j) // 2, k], (over_x, z))
 
     def rb1_copy(j, k):
-        return coded(rcode.at[j, k, 1], runit.at[j, k, 1], rfrom_y.at[j, k], rfrom_yu.at[j, k],
-                     rb1_send.at[j, k], rb1_recv.at[j, k], (over_y, z))
+        return coded(rcode.at[j, k, 1], runit.at[j, k, 1], rfrom_y.at[relayed_block(j) % 2, k], rfrom_yu.at[relayed_block(j) % 2, k],
+                     rb1_send.at[relayed_block(j) % 2, k], rb1_recv.at[relayed_block(j) % 2, k], (over_y, z))
 
     def ra2_copy(j, k):
         return coded(rcode.at[j, k, 0], runit.at[j, k, 0], rsum_y.at[k], rsum_yu.at[k],
@@ -328,13 +328,13 @@
         @when(both(jnp.logical_not(far_x), far_y))
         def _():
             ra1_copy(j, k).wait_recv()
-            encode(rpart[j, k, 0] + decode(rfrom_x[j, k], rfrom_xu[j, k]), rcode.at[j, k, 0], runit.at[j, k, 0])
+            encode(rpart[j, k, 0] + decode(rfrom_x[relayed_block(j) // 2, k], rfrom_xu[relayed_block(j) // 2, k]), rcode.at[j, k, 0], runit.at[j, k, 0])
             ra2_copy(j, k).start()
 
         @when(both(far_x, jnp.logical_not(far_y)))
         def _():
             rb1_copy(j, k).wait_recv()
-            encode(rpart[j, k, 1] + decode(rfrom_y[j, k], rfrom_yu[j, k]), rcode.at[j, k, 1], runit.at[j, k, 1])
+            encode(rpart[j, k, 1] + decode(rfrom_y[relayed_block(j) % 2, k], rfrom_yu[relayed_block(j) % 2, k]), rcode.at[j, k, 1], runit.at[j, k, 1])
             rb2_copy(j, k).start()
 
     def product(i):
@@ -358,6 +358,10 @@
                     share_copy(k).start()
                     rim[:, own_columns(k)] = got[b, k]
 
+            @when(both(inside, away == 2, k < relayed))
+            def _():
+                relay_product(depth - 2, k)
+
             for side in range(2):
                 stage(multiply(got[b, k], feats[:, side * half : (side + 1) * half]), (far_x, far_y)[side],
                       part.at[b, k, side], code.at[b, k, side], unit.at[b, k, side])
@@ -377,20 +381,16 @@
 
             lax.fori_loop(0, near * (depth - 2), lambda m, _: (relay_product(m // near, lax.rem(m, near)), 0)[1], 0)
 
-        @when(both(relay, k < relayed))
-        def _():
-            relay_product(depth - 2, k)
-
     home = (quad - z) * orient
 
     def hand_over(k):
         ra1_copy(home, k).wait_recv()
         ra2_copy(home, k).wait_recv()
-        encode(rpart[home, k, 0] + decode(rfrom_x[home, k], rfrom_xu[home, k]) + decode(rsum_y[k], rsum_yu[k]),
+        encode(rpart[home, k, 0] + decode(rfrom_x[y, k], rfrom_xu[y, k]) + decode(rsum_y[k], rsum_yu[k]),
                ready.at[k, :, 0:half], readyu.at[k, :, 0:half])
         rb1_copy(home, k).wait_recv()
         rb2_copy(home, k).wait_recv()
-        encode(rpart[home, k, 1] + decode(rfrom_y[home, k], rfrom_yu[home, k]) + decode(rsum_x[k], rsum_xu[k]),
+        encode(rpart[home, k, 1] + decode(rfrom_y[x, k], rfrom_yu[x, k]) + decode(rsum_x[k], rsum_xu[k]),
                ready.at[k, :, half : 2 * half], readyu.at[k, :, half : 2 * half])
         land_copy(k).start()
 
@@ -411,13 +411,13 @@
         @when(both(valid, jnp.logical_not(far_x), far_y))
         def _():
             a1_copy(b, k).wait_recv()
-            encode(part[b, k, 0] + decode(from_x[b, k], from_xu[b, k]), code.at[b, k, 0], unit.at[b, k, 0])
+            encode(part[b, k, 0] + decode(from_x[b // 2, k], from_xu[b // 2, k]), code.at[b, k, 0], unit.at[b, k, 0])
             a2_copy(b, k).start()
 
         @when(both(valid, far_x, jnp.logical_not(far_y)))
         def _():
             b1_copy(b, k).wait_recv()
-            encode(part[b, k, 1] + decode(from_y[b, k], from_yu[b, k]), code.at[b, k, 1], unit.at[b, k, 1])
+            encode(part[b, k, 1] + decode(from_y[b % 2, k], from_yu[b % 2, k]), code.at[b, k, 1], unit.at[b, k, 1])
             b2_copy(b, k).start()
 
         @when(gathered(i))
@@ -479,8 +479,8 @@
     def main(i, _):
         @when(both(i >= base, lax.rem(i, 2) == 0))
         def _():
+            combine(i - 1)
             combine(i - 2)
-            combine(i - 1)
 
         hand_over_early(i)
 
@@ -525,11 +525,11 @@
         def _():
             a1_copy(quad, k).wait_recv()
             a2_copy(quad, k).wait_recv()
-            o_ref[at, 0:half] = (part[quad, k, 0] + decode(from_x[quad, k], from_xu[quad, k])
+            o_ref[at, 0:half] = (part[quad, k, 0] + decode(from_x[y, k], from_xu[y, k])
                                  + decode(sum_y[k], sum_yu[k])) * scale
             b1_copy(quad, k).wait_recv()
             b2_copy(quad, k).wait_recv()
-            o_ref[at, half : 2 * half] = (part[quad, k, 1] + decode(from_y[quad, k], from_yu[quad, k])
+            o_ref[at, half : 2 * half] = (part[quad, k, 1] + decode(from_y[x, k], from_yu[x, k])
                                           + decode(sum_x[k], sum_xu[k])) * scale
 
         return 0
@@ -610,14 +610,14 @@
             pltpu.VMEM((2 * rows, width), inputs.dtype),
             pltpu.VMEM((depth, pieces, 2 * rows, LANES), inputs.dtype),
             pltpu.VMEM((depth, pieces, 2, LANES, half), f32),
-            pltpu.VMEM((depth, pieces, LANES, half), i16),
-            pltpu.VMEM((depth, pieces, LANES, half), i16),
+            pltpu.VMEM((2, pieces, LANES, half), i16),
+            pltpu.VMEM((2, pieces, LANES, half), i16),
             pltpu.VMEM((pieces, LANES, half), i16),
             pltpu.VMEM((pieces, LANES, half), i16),
             pltpu.VMEM((2 * rows, width), inputs.dtype),
             pltpu.VMEM((*outs, 2, LANES, half), f32),
-            pltpu.VMEM((*outs, LANES, half), i16),
-            pltpu.VMEM((*outs, LANES, half), i16),
+            pltpu.VMEM((2, relayed, LANES, half), i16),
+            pltpu.VMEM((2, relayed, LANES, half), i16),
             pltpu.VMEM((relayed, LANES, half), i16),
             pltpu.VMEM((relayed, LANES, half), i16),
             pltpu.VMEM((relayed, LANES, width), i16),
@@ -630,25 +630,26 @@
             pltpu.VMEM((width // LANES, LANES), f32),
             pltpu.VMEM((*grid, 2, LANES, half), i16),
             pltpu.VMEM((*grid, 2, 1, half), f32),
-            pltpu.VMEM((*grid, 1, half), f32),
-            pltpu.VMEM((*grid, 1, half), f32),
+            pltpu.VMEM((2, pieces, 1, half), f32),
+            pltpu.VMEM((2, pieces, 1, half), f32),
             pltpu.VMEM((pieces, 1, half), f32),
             pltpu.VMEM((pieces, 1, half), f32),
             pltpu.VMEM((*outs, 2, LANES, half), i16),
             pltpu.VMEM((*outs, 2, 1, half), f32),
-            pltpu.VMEM((*outs, 1, half), f32),
-            pltpu.VMEM((*outs, 1, half), f32),
+            pltpu.VMEM((2, relayed, 1, half), f32),
+            pltpu.VMEM((2, relayed, 1, half), f32),
             pltpu.VMEM((relayed, 1, half), f32),
             pltpu.VMEM((relayed, 1, half), f32),
             pltpu.SemaphoreType.DMA, dma(2), dma(peers), dma(peers), dma(2 * pieces), dma(2 * pieces),
             dma(pieces, 2), dma(pieces, 2), dma(*grid, 2), dma(*grid, 2),
-            dma(*grid, 2), dma(*grid, 2), dma(*grid, 2), dma(*grid, 2),
+            dma(2, pieces, 2), dma(2, pieces, 2), dma(2, pieces, 2), dma(2, pieces, 2),
             dma(pieces, 2), dma(pieces, 2), dma(pieces, 2), dma(pieces, 2),
-            dma(pieces), dma(pieces), dma(*outs, 2), dma(*outs, 2), dma(*outs, 2), dma(*outs, 2),
+            dma(pieces), dma(pieces),
+            dma(2, relayed, 2), dma(2, relayed, 2), dma(2, relayed, 2), dma(2, relayed, 2),
             dma(relayed, 2), dma(relayed, 2), dma(relayed, 2), dma(relayed, 2), dma(relayed, 2), dma(relayed, 2),
         ],
         compiler_params=pltpu.CompilerParams(collective_id=0, has_side_effects=True,
-                                             vmem_limit_bytes=63 * 1024 * 1024),
+                                             vmem_limit_bytes=52480 * 1024),
         name="gram",
     )(inputs, conv_weight, conv_bias.reshape(width // LANES, LANES), doc_start.reshape(rows // LANES, LANES), counts)
 

time: 126 us -> 121 us (0.960)
  Pallas kernels: 122 us -> 117 us
    pallas_call x1, Pallas kernels: 122 us -> 117 us  [fused_on_device(): pl.pallas_call(functools.partial(gram_kernel, peers, depth, taps, 1, rela...]
    unnamed x1 -> x7, local copies, waits for them, and re-layouts: 3.16 us -> 3.38 us
where the time goes in v2:
time: 121 us
  Pallas kernels  117 us (97%)
  local copies, waits for them, and re-layouts  3.38 us (3%)
    pallas_call x1, Pallas kernels, fused_on_device(): pl.pallas_call(functools.partial(gram_kernel, peers, depth, taps, 1, rela...  117 us
    unnamed x7, local copies, waits for them, and re-layouts  3.38 us

profile of v2, /device:TPU:6, one launch (start us, length us, event | category | flops | bytes accessed | tf_op | source)
XLA Modules:
  0.0 121.1 jit_solution(2680282528444216406)
XLA Ops:
  0.7 0.0 copy-start
  0.7 0.7 copy-done
  1.4 0.0 copy-start.1
  1.4 0.7 copy-done.1
  2.0 0.0 copy-start.2
  2.0 0.7 copy-done.2
  2.7 117.0 %gram.1 = f32[512,1024]{1,0:T(8,128)S(1)} custom-call(bf16[1024,1024]{1,0:T(8,128)(2,1)} %x_hbm.1, bf16[4,1024]{1,0:T(4,128)(2,1)S(1)} %copy-done, bf16[8,128]{1,0:T(8,128)(2,1)S(1)} %bitcast.3, s32[8,128]{1,0:T(8,128)S(1)} %bitcast.2, s32[1]{0:T(128)S(6)} %copy.7.counts_ref), custom_call_target="tpu_custom_call" | custom-call | tf_op jit(solution)/shard_map/gram/pallas_call | solution.py:603
  119.8 1.3 %copy.8 = f32[512,1024]{1,0:T(8,128)} copy(f32[512,1024]{1,0:T(8,128)S(1)} %gram.1) | data formatting | bytes 4194304
Async XLA Ops:
  0.7 0.7 copy-start
  1.4 0.7 copy-start.1
  2.0 0.7 copy-start.2

commit v3 on v2

--- a/solution.py
+++ b/solution.py
@@ -37,9 +37,9 @@
             copy.wait_recv()
 
 
-def gram_kernel(peers, depth, taps, near, relayed, x_hbm, taps_ref, bias_ref, doc_ref, counts_ref, o_ref, ext, feats, got, part,
+def gram_kernel(peers, depth, taps, near, relayed, x_hbm, taps_hbm, bias_hbm, doc_hbm, counts_ref, o_ref, ext, feats, got, part,
                 from_x, from_y, sum_y, sum_x, rim, rpart, rfrom_x, rfrom_y, rsum_y, rsum_x, ready, readyu, landed, landedu, totals,
-                lag_ref, cnt_ref, bias_rows, code, unit, from_xu, from_yu, sum_yu, sum_xu, rcode, runit, rfrom_xu, rfrom_yu, rsum_yu, rsum_xu,
+                lag_ref, cnt_ref, bias_rows, taps_ref, bias_ref, doc_ref, small_sem, code, unit, from_xu, from_yu, sum_yu, sum_xu, rcode, runit, rfrom_xu, rfrom_yu, rsum_yu, rsum_xu,
                 load_sem, halo_sem, cnt_send, cnt_recv, pair_send, pair_recv,
                 up_send, down_send, fwd_send, got_recv,
                 a1_send, a1_recv, b1_send, b1_recv, a2_send, a2_recv, b2_send, b2_recv,
@@ -69,6 +69,10 @@
 
     load = pltpu.make_async_copy(x_hbm, ext.at[pl.ds(HALO, rows)], load_sem)
     load.start()
+    small = [pltpu.make_async_copy(src, dst, small_sem.at[n]) for n, (src, dst) in
+             enumerate(((doc_hbm, doc_ref), (bias_hbm, bias_ref), (taps_hbm, taps_ref)))]
+    for copy in small:
+        copy.start()
 
     barrier = pltpu.get_barrier_semaphore()
     for step in range(1, peers):
@@ -81,6 +85,9 @@
     @when(z < depth - 1)
     def _():
         pl.semaphore_signal(barrier, inc=1, device_id=(s, z + 1), device_id_type=MESH)
+
+    for copy in small:
+        copy.wait()
 
     bias_rows[...] = bias_ref[...].astype(jnp.float32)
     cnt_ref[...] = jnp.broadcast_to(counts_ref[0], cnt_ref.shape)
@@ -400,7 +407,7 @@
             lax.fori_loop(0, near, lambda k, _: (hand_over(k), 0)[1], 0)
 
         for k in range(relayed):
-            @when(both(inside, home == depth - 2, i == base + 4 + 3 * k))
+            @when(both(inside, home == depth - 2, i == base + (2, 7)[k]))
             def _():
                 hand_over(k)
 
@@ -557,7 +564,7 @@
     for step in range(1, peers):
         cnt_copy(step, s).wait_send()
 
-    lax.fori_loop(steps - base, steps, sent_late, 0)
+    lax.fori_loop((steps - base) // 2, steps // 2, lambda n, _: sent_late(2 * n, 0), 0)
 
     def sent_relayed(m, _):
         j, k = m // relayed, lax.rem(m, relayed)
@@ -586,7 +593,9 @@
 
         return 0
 
-    lax.fori_loop(0, relayed * (depth - 1), sent_relayed, 0)
+    @when(inside)
+    def _():
+        lax.fori_loop(0, relayed * (depth - 1), sent_relayed, 0)
 
 
 def fused_on_device(peers, depth, inputs, conv_weight, conv_bias, doc_start, counts):
@@ -603,7 +612,7 @@
     return pl.pallas_call(
         functools.partial(gram_kernel, peers, depth, taps, 1, relayed),
         out_shape=jax.ShapeDtypeStruct((half, width), f32),
-        in_specs=[pl.BlockSpec(memory_space=pl.ANY), vmem, vmem, vmem, pl.BlockSpec(memory_space=pltpu.SMEM)],
+        in_specs=[pl.BlockSpec(memory_space=pl.ANY)] * 4 + [ pl.BlockSpec(memory_space=pltpu.SMEM)],
         out_specs=vmem,
         scratch_shapes=[
             pltpu.VMEM((rows + HALO, width), inputs.dtype),
@@ -628,6 +637,10 @@
             pltpu.VMEM((rows, LANES), jnp.int32),
             pltpu.VMEM((8, LANES), jnp.int32),
             pltpu.VMEM((width // LANES, LANES), f32),
+            pltpu.VMEM(conv_weight.shape, conv_weight.dtype),
+            pltpu.VMEM((width // LANES, LANES), conv_bias.dtype),
+            pltpu.VMEM((rows // LANES, LANES), doc_start.dtype),
+            dma(3),
             pltpu.VMEM((*grid, 2, LANES, half), i16),
             pltpu.VMEM((*grid, 2, 1, half), f32),
             pltpu.VMEM((2, pieces, 1, half), f32),
@@ -651,7 +664,7 @@
         compiler_params=pltpu.CompilerParams(collective_id=0, has_side_effects=True,
                                              vmem_limit_bytes=52480 * 1024),
         name="gram",
-    )(inputs, conv_weight, conv_bias.reshape(width // LANES, LANES), doc_start.reshape(rows // LANES, LANES), counts)
+    )(inputs, *(pltpu.with_memory_space_constraint(a, pltpu.HBM) for a in (conv_weight, conv_bias.reshape(width // LANES, LANES), doc_start.reshape(rows // LANES, LANES))), counts)
 
 
 def passed_along(x, axis, by):

time: 121 us -> 119 us (0.983)
  local copies, waits for them, and re-layouts: 3.38 us -> 1.32 us
    unnamed x7 -> x1, local copies, waits for them, and re-layouts: 3.38 us -> 1.32 us
where the time goes in v3:
time: 119 us
  Pallas kernels  117 us (98%)
  local copies, waits for them, and re-layouts  1.32 us (1%)
    pallas_call x1, Pallas kernels, fused_on_device(): pl.pallas_call(functools.partial(gram_kernel, peers, depth, taps, 1, rela...  117 us

profile of v3, /device:TPU:6, one launch (start us, length us, event | category | flops | bytes accessed | tf_op | source)
XLA Modules:
  0.0 118.5 jit_solution(12213533460494891643)
XLA Ops:
  0.7 116.6 %gram.1 = f32[512,1024]{1,0:T(8,128)S(1)} custom-call(bf16[1024,1024]{1,0:T(8,128)(2,1)} %x_hbm.1, bf16[4,1024]{1,0:T(4,128)(2,1)} %taps_hbm.1, bf16[8,128]{1,0:T(8,128)(2,1)} %bitcast.3, s32[8,128]{1,0:T(8,128)} %bitcast.2, s32[1]{0:T(128)S(6)} %copy.7.counts_ref), custom_call_target="tpu_custom_call" | custom-call | tf_op jit(solution)/shard_map/gram/pallas_call | solution.py:612
  117.2 1.3 %copy.8 = f32[512,1024]{1,0:T(8,128)} copy(f32[512,1024]{1,0:T(8,128)S(1)} %gram.1) | data formatting | bytes 4194304

commit v4 on v3

--- a/solution.py
+++ b/solution.py
@@ -152,15 +152,21 @@
         return pl.ds(pl.multiple_of(core * half + k * LANES, LANES), LANES)
 
     def tokens(j):
-        return pl.ds(pl.multiple_of(j * rows, rows), rows)
+        return pl.ds(pl.multiple_of(j * (rows // 2), rows // 2), rows // 2)
+
+    def chunks(of):
+        return 2 * of, 2 * of + 1
 
     def up_copy(k, j):
-        return remote(feats.at[tokens(j), own_columns(k)], got.at[z, k, tokens(j)], up_send.at[k, j],
+        return remote(feats.at[tokens(j), own_columns(k)], got.at[z, k, tokens(j)], up_send.at[k],
                       got_recv.at[z, k, j], (s, lax.rem(z + 1, depth)))
 
     def down_copy(k, j):
-        return remote(feats.at[tokens(j), own_columns(k)], got.at[z, k, tokens(j)], down_send.at[k, j],
+        return remote(feats.at[tokens(j), own_columns(k)], got.at[z, k, tokens(j)], down_send.at[k],
                       got_recv.at[z, k, j], (s, lax.rem(z + depth - 1, depth)))
+
+    def piece_sent(k, send):
+        remote(got.at[z, k], got.at[z, k], send, got_recv.at[z, k, 0], (s, lax.rem(z + 1, depth))).wait_send()
 
     def goes_up(k):
         return either(z < depth - 2, both(z == depth - 2, k >= near))
@@ -169,8 +175,17 @@
         return either(z > 1, both(z == 1, k >= near))
 
     blocks = rows // block
-    for side in (1 - core, core):
-        conv(side * half, 1, blocks)
+    conv(core * half, 1, blocks)
+
+    @when(goes_up(0))
+    def _():
+        up_copy(0, 2 * core + 1).start()
+
+    @when(goes_down(0))
+    def _():
+        down_copy(0, 2 * core + 1).start()
+
+    conv((1 - core) * half, 1, blocks)
 
     @when(s == 0)
     def _():
@@ -187,14 +202,17 @@
             pair_copy(piece, own_rows).start()
 
 
-        def send(j):
-            @when(goes_up(k))
-            def _():
-                up_copy(k, j).start()
-
-            @when(goes_down(k))
-            def _():
-                down_copy(k, j).start()
+        def send(of):
+            for n, j in enumerate(chunks(of)):
+                due = either(k > 0, of != core) if n else True
+
+                @when(both(goes_up(k), due))
+                def _():
+                    up_copy(k, j).start()
+
+                @when(both(goes_down(k), due))
+                def _():
+                    down_copy(k, j).start()
 
         make(1 - core)
         make(core)
@@ -243,7 +261,7 @@
 
     def fwd_copy(block_at, k, j, sign):
         to = lax.rem(z - sign + depth, depth)
-        return remote(got.at[block_at, k, tokens(j)], got.at[block_at, k, tokens(j)], fwd_send.at[block_at, k, j],
+        return remote(got.at[block_at, k, tokens(j)], got.at[block_at, k, tokens(j)], fwd_send.at[block_at, k],
                       got_recv.at[block_at, k, j], (s, to))
 
     def coded(src, srcu, dst, dstu, send, recv, to):
@@ -353,7 +371,7 @@
         def _():
             @when(away > 0)
             def _():
-                for j in (core, 1 - core):
+                for j in (*chunks(core), *chunks(1 - core)):
                     fwd_copy(b, k, j, sign).wait_recv()
 
                     @when(passes)
@@ -407,7 +425,7 @@
             lax.fori_loop(0, near, lambda k, _: (hand_over(k), 0)[1], 0)
 
         for k in range(relayed):
-            @when(both(inside, home == depth - 2, i == base + (2, 7)[k]))
+            @when(both(inside, home == depth - 2, i == base + (2, 6, 7)[k]))
             def _():
                 hand_over(k)
 
@@ -441,14 +459,13 @@
         for side in range(2):
             pair_copy(side * pieces + k, own_rows).wait_send()
 
-        for j in range(2):
-            @when(goes_up(k))
-            def _():
-                up_copy(k, j).wait_send()
-
-            @when(goes_down(k))
-            def _():
-                down_copy(k, j).wait_send()
+        @when(goes_up(k))
+        def _():
+            piece_sent(k, up_send.at[k])
+
+        @when(goes_down(k))
+        def _():
+            piece_sent(k, down_send.at[k])
 
         @when(inside)
         def _():
@@ -462,8 +479,7 @@
 
         @when(onward(away, k, sign, valid))
         def _():
-            for j in range(2):
-                fwd_copy(b, k, j, sign).wait_send()
+            piece_sent(k, fwd_send.at[b, k])
 
         @when(both(valid, far_x))
         def _():
@@ -603,7 +619,7 @@
     taps = conv_weight.shape[0]
     half = width // 2
     pieces = half // LANES
-    relayed = pieces // 2
+    relayed = 3
     vmem = pl.BlockSpec(memory_space=pltpu.VMEM)
     dma = lambda *shape: pltpu.SemaphoreType.DMA(shape)
     f32, i16 = jnp.float32, jnp.int16
@@ -654,7 +670,7 @@
             pltpu.VMEM((relayed, 1, half), f32),
             pltpu.VMEM((relayed, 1, half), f32),
             pltpu.SemaphoreType.DMA, dma(2), dma(peers), dma(peers), dma(2 * pieces), dma(2 * pieces),
-            dma(pieces, 2), dma(pieces, 2), dma(*grid, 2), dma(*grid, 2),
+            dma(pieces), dma(pieces), dma(*grid), dma(*grid, 4),
             dma(2, pieces, 2), dma(2, pieces, 2), dma(2, pieces, 2), dma(2, pieces, 2),
             dma(pieces, 2), dma(pieces, 2), dma(pieces, 2), dma(pieces, 2),
             dma(pieces), dma(pieces),

time: 119 us -> 118 us (level)
  no operation moved by 1% of the time
where the time goes in v4:
time: 118 us
  Pallas kernels  116 us (98%)
  local copies, waits for them, and re-layouts  1.32 us (1%)
    pallas_call x1, Pallas kernels, fused_on_device(): pl.pallas_call(functools.partial(gram_kernel, peers, depth, taps, 1, rela...  116 us

profile of v4, /device:TPU:6, one launch (start us, length us, event | category | flops | bytes accessed | tf_op | source)
XLA Modules:
  0.0 117.7 jit_solution(7755519296036050947)
XLA Ops:
  0.7 115.8 %gram.1 = f32[512,1024]{1,0:T(8,128)S(1)} custom-call(bf16[1024,1024]{1,0:T(8,128)(2,1)} %x_hbm.1, bf16[4,1024]{1,0:T(4,128)(2,1)} %taps_hbm.1, bf16[8,128]{1,0:T(8,128)(2,1)} %bitcast.3, s32[8,128]{1,0:T(8,128)} %bitcast.2, s32[1]{0:T(128)S(6)} %copy.7.counts_ref), custom_call_target="tpu_custom_call" | custom-call | tf_op jit(solution)/shard_map/gram/pallas_call | solution.py:628
  116.4 1.3 %copy.8 = f32[512,1024]{1,0:T(8,128)} copy(f32[512,1024]{1,0:T(8,128)S(1)} %gram.1) | data formatting | bytes 4194304
